TPU v7x, 256 devices: a whole 4x4x8 slice. The times are simulated.
256 devices in a mesh: dp: 4 (over x), expert: 64 (over y, z, core).
Axes of the slice: x: 4, y: 4, z: 8, core: 2. Of those that a mesh axis runs over, the one named last changes fastest.
Arguments:
- hidden: bfloat16 [4, 4096, 2, 2048], P('dp', 'expert'), may hold values from -6 to 6
- queries: bfloat16 [4, 4096, 2, 4096], P('dp', 'expert'), may hold values from -45 to 45
- latents: bfloat16 [4, 4096, 2, 512], P('dp', 'expert'), may hold values from -165 to 165
- mem_latents: bfloat16 [4, 32, 2, 512], P('dp'), may hold values from -6 to 6
- lengths: int32 [4, 2], P('dp'), may hold values from 2048 to 4096
- ids: int32 [4, 4096, 2, 6], P('dp', 'expert'), may hold values from 0 to 63, all different within a row; in each aligned block of 128 rows (0 to 127, 128 to 255, ..., all dimensions but the last counted through in order) at most 14 rows name the same one
- gates: bfloat16 [4, 4096, 2, 6], P('dp', 'expert'), may hold values from 0.049804688 to 0.5
- norm_gain: bfloat16 [2048], replicated, may hold values from 0.25 to 1.75
- w_uv: bfloat16 [8, 512, 128], P('dp'), may hold values from -0.25 to 0.25
- w_out: bfloat16 [1024, 2048], P('dp'), may hold values from -0.1875 to 0.1875
- w_gate: bfloat16 [64, 2048, 704], P('expert'), may hold values from -0.125 to 0.125
- w_up: bfloat16 [64, 2048, 704], P('expert'), may hold values from -0.125 to 0.125
- w_down: bfloat16 [64, 704, 2048], P('expert'), may hold values from -0.21875 to 0.21875
Outputs:
- layer_out: bfloat16 [4, 4096, 2, 2048], P('dp', 'expert')
Inputs may be any that keep to these rules, and one draw needn't show every extreme that they name: `ids`: each row names 6 different experts; the rows of one device (aligned blocks of 128 rows in the order of the leading dimensions) name any one expert at most 14 times, a bound that some block reaches.
All inputs are finite; a program needn't handle non-finite values.
Results may differ from a plain program's by a relative error of at most 0.007.
Values may be sent and summed in bfloat16 or wider, within the bound.
A program may use at most 128 MiB of HBM per device.

v0:
```python
import jax
import jax.numpy as jnp
from jax import lax
from jax.sharding import PartitionSpec as P

score_scale = 192.0 ** (-0.5)
norm_eps = 1e-06


def sent_to_all(shard, axis):
    devices = lax.axis_size(axis)
    return lax.all_to_all(
        jnp.broadcast_to(shard[None], (devices, *shard.shape)), axis, 0, 0, tiled=True
    )


def joined_along(blocks, dim):
    dims = list(blocks.shape[1:])
    dims[dim] *= blocks.shape[0]
    return jnp.moveaxis(blocks, 0, dim).reshape(dims)


def gather_directly(shard, axis, dim):
    blocks = sent_to_all(shard, axis)
    return joined_along(blocks, dim)


def shards(
    hidden,
    queries,
    latents,
    mem_latents,
    lengths,
    ids,
    gates,
    norm_gain,
    w_uv,
    w_out,
    w_gate,
    w_up,
    w_down,
):
    local_len = hidden.shape[1]
    seq_count = hidden.shape[2]
    model_width = hidden.shape[3]
    latent_dim = latents.shape[3]
    head_count = queries.shape[3] // latent_dim
    row_count = local_len * seq_count
    owner_count = lax.axis_size("expert")
    shard_index = lax.axis_index("expert")
    own_pos = shard_index * local_len + jnp.arange(local_len, dtype=jnp.int32)
    query_rows = queries[0].reshape(local_len, seq_count, head_count, latent_dim)
    memory = mem_latents[0]
    seq_limit = lengths[0]
    mem_scores = (
        jnp.einsum("tshl,msl->shtm", query_rows, memory, preferred_element_type=jnp.float32)
        * score_scale
    )
    first_max = jnp.max(mem_scores, axis=3)
    mem_weights = jnp.exp(mem_scores - first_max[..., None])
    first_sum = jnp.sum(mem_weights, axis=3)
    first_acc = jnp.einsum(
        "shtm,msl->tshl",
        mem_weights.astype(jnp.bfloat16),
        memory,
        preferred_element_type=jnp.float32,
    )

    def fold_step(carry, portion):
        old_max, old_sum, old_acc = carry
        key_rows = portion[0]
        key_pos = jnp.arange(key_rows.shape[0], dtype=jnp.int32)
        scores = (
            jnp.einsum("tshl,jsl->shtj", query_rows, key_rows, preferred_element_type=jnp.float32)
            * score_scale
        )
        causal = key_pos[None, :] <= own_pos[:, None]
        inside = key_pos[None, :] < seq_limit[:, None]
        visible = causal[None, None, :, :] & inside[:, None, None, :]
        scores = jnp.where(visible, scores, -jnp.inf)
        new_max = jnp.maximum(old_max, jnp.max(scores, axis=3))
        weights = jnp.exp(scores - new_max[..., None])
        factor = jnp.exp(old_max - new_max)
        new_sum = old_sum * factor + jnp.sum(weights, axis=3)
        contrib = jnp.einsum(
            "shtj,jsl->tshl",
            weights.astype(jnp.bfloat16),
            key_rows,
            preferred_element_type=jnp.float32,
        )
        new_acc = old_acc * jnp.transpose(factor, (2, 0, 1))[..., None] + contrib
        return (new_max, new_sum, new_acc)

    portion = lax.all_gather(latents, "expert", axis=1, tiled=True)
    last_pos = jnp.max(own_pos)
    final_max, final_sum, final_acc = lax.cond(
        jnp.int32(0) <= last_pos,
        lambda state: fold_step(state, portion),
        lambda state: state,
        (first_max, first_sum, first_acc),
    )
    attended = (final_acc / jnp.transpose(final_sum, (2, 0, 1))[..., None]).astype(jnp.bfloat16)
    values = jnp.einsum(
        "tshl,hlv->tshv",
        attended,
        gather_directly(w_uv, "dp", 0),
        preferred_element_type=jnp.float32,
    ).astype(jnp.bfloat16)
    flat_values = values.reshape(row_count, -1)
    attn_out = jnp.dot(
        flat_values,
        lax.all_gather(w_out, "dp", axis=0, tiled=True),
        preferred_element_type=jnp.float32,
    )
    residual = hidden[0].reshape(row_count, model_width).astype(jnp.float32) + attn_out
    mean_square = jnp.mean(residual * residual, axis=-1, keepdims=True)
    normed = (residual * lax.rsqrt(mean_square + norm_eps) * norm_gain.astype(jnp.float32)).astype(
        jnp.bfloat16
    )
    experts_here = w_gate.shape[0]
    expert_count = owner_count * experts_here
    top_count = ids.shape[3]
    capacity = min(row_count, row_count * top_count // expert_count + 2)
    flat_ids = ids[0].reshape(row_count * top_count)
    onehot = (flat_ids[:, None] == jnp.arange(expert_count, dtype=jnp.int32)[None, :]).astype(
        jnp.int32
    )
    before = jnp.cumsum(onehot, axis=0) - onehot
    slot_within = jnp.sum(before * onehot, axis=1)
    slot_index = (flat_ids * capacity + slot_within).reshape(row_count, top_count)
    matching = (
        jnp.arange(expert_count * capacity, dtype=jnp.int32)[:, None, None]
        == slot_index[None, :, :]
    )
    placing = jnp.any(matching, axis=2).astype(jnp.bfloat16)
    gate_rows = gates[0].reshape(row_count, top_count).astype(jnp.float32)
    mixing = jnp.sum(jnp.where(matching, gate_rows[None, :, :], jnp.float32(0.0)), axis=2).astype(
        jnp.bfloat16
    )
    outgoing = jnp.dot(placing, normed, preferred_element_type=jnp.float32).astype(jnp.bfloat16)
    outgoing = outgoing.reshape(owner_count, experts_here, capacity, model_width)
    incoming = lax.all_to_all(outgoing, "expert", split_axis=0, concat_axis=0, tiled=True)
    gate_h = jnp.einsum("necd,edf->necf", incoming, w_gate, preferred_element_type=jnp.float32)
    up_h = jnp.einsum("necd,edf->necf", incoming, w_up, preferred_element_type=jnp.float32)
    act = (jax.nn.silu(gate_h) * up_h).astype(jnp.bfloat16)
    produced = jnp.einsum("necf,efd->necd", act, w_down, preferred_element_type=jnp.float32).astype(
        jnp.bfloat16
    )
    returned = lax.all_to_all(produced, "expert", split_axis=0, concat_axis=0, tiled=True)
    combined_rows = returned.reshape(expert_count * capacity, model_width)
    routed = jnp.einsum("st,sd->td", mixing, combined_rows, preferred_element_type=jnp.float32)
    layer_out = (residual + routed).astype(jnp.bfloat16)
    return layer_out.reshape(1, local_len, seq_count, model_width)


def solution(mesh):
    return jax.shard_map(
        shards,
        mesh=mesh,
        in_specs=(
            P("dp", "expert", None, None),
            P("dp", "expert", None, None),
            P("dp", "expert", None, None),
            P("dp", None, None, None),
            P("dp", None),
            P("dp", "expert", None, None),
            P("dp", "expert", None, None),
            P(),
            P("dp", None, None),
            P("dp", None),
            P("expert", None, None),
            P("expert", None, None),
            P("expert", None, None),
        ),
        out_specs=P("dp", "expert", None, None),
        check_vma=False,
    )
```

profile of v0, /device:TPU:1, one launch (start us, length us, event | category | flops | bytes accessed | tf_op | source)
XLA Modules:
  0.0 415.4 jit_solution(3627106416608245663)
XLA Ops:
  9.0 2.1 broadcast_in_dim.29
  11.1 4.8 %all-to-all-start = ((bf16[4,2,512,128]{3,2,1,0:T(8,128)(2,1)}), bf16[4,2,512,128]{3,2,1,0:T(8,128)(2,1)}, u32[]{:S(2)}, u32[]{:S(2)}) async-start(bf16[4,2,512,128]{3,2,1,0:T(8,128)(2,1)} %broadcast_in_dim.29), calls=%async_computation | async-start | bytes 2097152 | tf_op jit(solution)/shard_map/all_to_all | solution.py:12
  16.4 2.6 reshape.151
  23.9 2.5 fusion.69
  26.7 2.7 convolution_bitcast_fusion
  29.9 67.4 %all-gather.3.cloned.1.call-done = bf16[1,4096,2,512]{3,1,2,0:T(8,128)(2,1)} async-done(((bf16[1,64,2,512]{3,1,2,0:T(8,128)(2,1)}), bf16[1,4096,2,512]{3,1,2,0:T(8,128)(2,1)}) %all-gather.3.cloned.1.call-update) | async-done | bytes 8388624 | tf_op jit(solution)/shard_map/all_gather | solution.py:94
  97.3 38.6 %conditional.1 = ((f32[2,8,64]{2,1,0:T(8,128)S(1)}, f32[64,2,8,512]{3,0,2,1:T(8,128)})) conditional(s32[]{:T(128)} %convert_element_type.74, (f32[2,8,64]{2,1,0:T(8,128)S(1)}, f32[64,2,8,512]{3,0,2,1:T(8,128)}) %tuple.12, (s32[64]{0:T(128)S(1)}, s32[1,2]{1,0:T(1,128)}, bf16[1,4096,2,512]{3,1,2,0:T(8,128)(2,1)}, bf16[64,2,8,512]{3,2,1,0:T(8,128)(2,1)}, ...), branch_computations={%region_3.0_spmd, %region_4.7_spmd} | conditional | flops 8637918208 | bytes 75047200 | solution.py:96
  98.6 15.8 %fusion.2 = (f32[2,8,64]{2,1,0:T(8,128)}, f32[2,4096,64,8]{1,2,3,0:T(8,128)}) fusion(pred[2,64,4096]{2,1,0:T(8,128)(4,1)S(1)} %broadcast_and_fusion, bf16[64,2,8,512]{3,2,1,0:T(8,128)(2,1)} %get-tuple-element.57, bf16[1,4096,2,512]{3,1,2,0:T(8,128)(2,1)} %get-tuple-element.27), kind=kOutput, calls=%fused_computation.4 | convolution fusion | flops 4307549184 | bytes 26742784 | tf_op jit(solution)/shard_map/cond/branch_1_fun/tshl,jsl->shtj/dot_general | solution.py:74
  115.1 12.4 %bitcast_add_fusion = f32[64,2,8,512]{3,0,2,1:T(8,128)} fusion(f32[64,2,8,512]{3,0,2,1:T(8,128)} %get-tuple-element.29, bf16[1,4096,2,512]{3,1,2,0:T(8,128)(2,1)} %get-tuple-element.27, f32[2,4096,64,8]{1,2,3,0:T(8,128)} %get-tuple-element.61, f32[2,8,64]{2,1,0:T(8,128)S(1)} %get-tuple-element.59, pred[2,64,4096]{2,1,0:T(8,128)(4,1)S(1)} %broadcast_and_fusion, ...), kind=kOutput, calls=%fused_computation.13 | convolution fusion | flops 4312793088 | bytes 29892608 | tf_op jit(solution)/shard_map/cond/branch_1_fun/shtj,jsl->tshl/dot_general | solution.py:85
  127.5 8.4 %fusion.1 = f32[2,8,64]{2,1,0:T(8,128)S(1)} fusion(f32[2,4096,64,8]{1,2,3,0:T(8,128)} %get-tuple-element.61, f32[2,8,64]{2,1,0:T(8,128)S(1)} %get-tuple-element.59, pred[2,64,4096]{2,1,0:T(8,128)(4,1)S(1)} %broadcast_and_fusion), kind=kLoop, calls=%fused_computation.3 | loop fusion | flops 16776192 | bytes 17309696 | tf_op jit(solution)/shard_map/cond/branch_1_fun/reduce_sum | solution.py:84
  135.9 2.4 fusion.48
  138.5 7.6 %all-gather.5.cloned.1.call-done = bf16[1024,2048]{1,0:T(8,128)(2,1)} async-done(((bf16[256,2048]{1,0:T(8,128)(2,1)}), bf16[1024,2048]{1,0:T(8,128)(2,1)}) %all-gather.5.cloned.1.call-update) | async-done | bytes 4194320 | tf_op jit(solution)/shard_map/all_gather | solution.py:112
  146.1 3.3 multiply_reduce_fusion
  150.4 3.0 convolution_convert_fusion
  153.4 6.0 %reshape.134 = bf16[64,1,14,2048]{3,2,0,1:T(8,128)(2,1)} reshape(bf16[896,2048]{1,0:T(8,128)(2,1)} %convolution_convert_fusion) | data formatting | bytes 7340032 | tf_op jit(solution)/shard_map/reshape | solution.py:141
  159.4 107.3 %all_to_all.15 = bf16[64,1,14,2048]{3,2,1,0:T(8,128)(2,1)S(1)} all-to-all(bf16[64,1,14,2048]{3,2,1,0:T(8,128)(2,1)} %bitcast.151), channel_id=1, replica_groups=mesh['dp'=4,'expert'=64] {'expert'}, dimensions={0} | all-to-all | bytes 7340032 | tf_op jit(solution)/shard_map/all_to_all | solution.py:142
  266.7 1.9 copy-done.2
  268.6 8.7 %fusion.22 = f32[64,14,704]{2,0,1:T(8,128)} fusion(bf16[64,1,14,2048]{3,2,1,0:T(8,128)(2,1)S(1)} %all_to_all.15, bf16[1,2048,704]{1,2,0:T(8,128)(2,1)S(1)} %copy-done.7), kind=kOutput, calls=%fused_computation.25 | convolution fusion | flops 2583691264 | bytes 9076736 | tf_op jit(solution)/shard_map/necd,edf->necf/dot_general | solution.py:143
  277.3 12.9 %convert_bitcast_fusion = bf16[64,1,14,2048]{3,0,2,1:T(8,128)(2,1)} fusion(bf16[1,704,2048]{2,1,0:T(8,128)(2,1)S(1)} %copy-done, bf16[1,2048,704]{1,2,0:T(8,128)(2,1)} %param.26, bf16[64,1,14,2048]{3,2,1,0:T(8,128)(2,1)} %copy-done.2, f32[64,14,704]{2,0,1:T(8,128)} %fusion.22), kind=kOutput, calls=%fused_computation.27 | convolution fusion | flops 5173002240 | bytes 15630336 | tf_op jit(solution)/shard_map/necf,efd->necd/dot_general | solution.py:146
  290.2 6.0 %copy.68 = bf16[64,1,14,2048]{3,2,1,0:T(8,128)(2,1)} copy(bf16[64,1,14,2048]{3,0,2,1:T(8,128)(2,1)} %convert_bitcast_fusion) | data formatting | bytes 7340032 | tf_op jit(solution)/shard_map/convert_element_type | solution.py:146
  296.2 6.2 %all-to-all-start.2 = ((bf16[64,1,14,2048]{3,2,1,0:T(8,128)(2,1)}), bf16[64,1,14,2048]{3,2,1,0:T(8,128)(2,1)}, u32[]{:S(2)}, u32[]{:S(2)}) async-start(bf16[64,1,14,2048]{3,2,1,0:T(8,128)(2,1)} %copy.68), calls=%async_computation.2 | async-start | bytes 8388608 | tf_op jit(solution)/shard_map/all_to_all | solution.py:149
  303.6 94.6 %all-to-all-done.2 = bf16[64,1,14,2048]{3,2,1,0:T(8,128)(2,1)} async-done(((bf16[64,1,14,2048]{3,2,1,0:T(8,128)(2,1)}), bf16[64,1,14,2048]{3,2,1,0:T(8,128)(2,1)}, u32[]{:S(2)}, u32[]{:S(2)}) %all-to-all-start.2) | async-done | bytes 3670048 | tf_op jit(solution)/shard_map/all_to_all | solution.py:149
  398.3 6.0 %reshape.140 = bf16[896,2048]{1,0:T(8,128)(2,1)} reshape(bf16[64,1,14,2048]{3,2,1,0:T(8,128)(2,1)} %all-to-all-done.2) | data formatting | bytes 7340032 | tf_op jit(solution)/shard_map/reshape | solution.py:150
  404.2 3.1 fusion.34
  (51 shorter events, 13.3 us)
Async XLA Ops:
  6.5 270.8 %copy-start = (bf16[1,704,2048]{2,1,0:T(8,128)(2,1)S(1)}, bf16[1,704,2048]{2,1,0:T(8,128)(2,1)}, u32[]{:S(2)}) copy-start(bf16[1,704,2048]{2,1,0:T(8,128)(2,1)} %param.27) | copy-start | bytes 8650756
  6.5 9.4 %copy-start.4 = (s32[1,64,2,6]{1,2,3,0:T(2,128)S(1)}, s32[1,64,2,6]{1,2,3,0:T(2,128)}, u32[]{:S(2)}) copy-start(s32[1,64,2,6]{1,2,3,0:T(2,128)} %param.20) | copy-start | bytes 9220
  6.5 13.8 %copy-start.3 = (bf16[1,64,2,2048]{3,2,1,0:T(2,128)(2,1)S(1)}, bf16[1,64,2,2048]{3,2,1,0:T(2,128)(2,1)}, u32[]{:S(2)}) copy-start(bf16[1,64,2,2048]{3,2,1,0:T(2,128)(2,1)} %param.15) | copy-start | bytes 1572868
  6.5 90.8 %all-gather.3.cloned.1.call-start = ((), (), s32[]{:S(2)}) async-start(), calls=%async_computation.3 | async-start | bytes 8519680 | tf_op jit(solution)/shard_map/all_gather | solution.py:94
  8.3 137.8 %all-gather.5.cloned.1.call-start = ((), (), s32[]{:S(2)}) async-start(), calls=%async_computation.4 | async-start | bytes 5242880 | tf_op jit(solution)/shard_map/all_gather | solution.py:112
  11.1 124.8 %all-to-all-start = ((bf16[4,2,512,128]{3,2,1,0:T(8,128)(2,1)}), bf16[4,2,512,128]{3,2,1,0:T(8,128)(2,1)}, u32[]{:S(2)}, u32[]{:S(2)}) async-start(bf16[4,2,512,128]{3,2,1,0:T(8,128)(2,1)} %broadcast_in_dim.29), calls=%async_computation | async-start | bytes 2097152 | tf_op jit(solution)/shard_map/all_to_all | solution.py:12
  16.0 10.7 %copy-start.5 = (bf16[2048]{0:T(1024)(128)(2,1)S(1)}, bf16[2048]{0:T(1024)(128)(2,1)}, u32[]{:S(2)}) copy-start(bf16[2048]{0:T(1024)(128)(2,1)} %param.22) | copy-start | bytes 12292
  149.4 1.0 copy-start.1
  159.4 109.2 %copy-start.7 = (bf16[1,2048,704]{1,2,0:T(8,128)(2,1)S(1)}, bf16[1,2048,704]{1,2,0:T(8,128)(2,1)}, u32[]{:S(2)}) copy-start(bf16[1,2048,704]{1,2,0:T(8,128)(2,1)} %param.25) | copy-start | bytes 8650756
  266.7 1.9 copy-start.2
  296.2 6.2 %copy-start.6 = (bf16[1,64,2,6]{1,2,3,0:T(2,128)(2,1)S(1)}, bf16[1,64,2,6]{1,2,3,0:T(2,128)(2,1)}, u32[]{:S(2)}) copy-start(bf16[1,64,2,6]{1,2,3,0:T(2,128)(2,1)} %param.21) | copy-start | bytes 4612
  296.2 102.0 %all-to-all-start.2 = ((bf16[64,1,14,2048]{3,2,1,0:T(8,128)(2,1)}), bf16[64,1,14,2048]{3,2,1,0:T(8,128)(2,1)}, u32[]{:S(2)}, u32[]{:S(2)}) async-start(bf16[64,1,14,2048]{3,2,1,0:T(8,128)(2,1)} %copy.68), calls=%async_computation.2 | async-start | bytes 8388608 | tf_op jit(solution)/shard_map/all_to_all | solution.py:149
Sparse Core Ops, SparseCore 0:
  10.1 87.1 all-gather.2
  99.1 46.9 all-gather.4
where the time goes:
time: 416 us; the launch traced here: 415 us
  waiting for transfers between devices  170 us (41%)
  blocking collectives  107 us (26%)
  matrix products  66.9 us (16%)
  local copies, waits for them, and re-layouts  30.9 us (7%)
  other arithmetic  14.6 us (4%)
  between operations  14.2 us (3%)
  starting transfers between devices  11.1 us (3%)
    all_to_all x1, blocking collectives, shards(): lax.all_to_all(outgoing, 'expert', split_axis=0, concat_axis=0, tiled=True)  107 us
    all_to_all x1, waiting for transfers between devices, shards(): lax.all_to_all(produced, 'expert', split_axis=0, concat_axis=0, tiled=True)  94.6 us
    all_gather x1, waiting for transfers between devices, shards(): portion = lax.all_gather(latents, 'expert', axis=1, tiled=True)  67.4 us
    dot_general x1, matrix products, fold_step(): jnp.einsum('tshl,jsl->shtj', query_rows, key_rows, preferred_element_type...  15.8 us
    dot_general x1, matrix products, shards(): jnp.einsum('necf,efd->necd', act, w_down, preferred_element_type=jnp.floa...  12.9 us
    dot_general x1, matrix products, fold_step(): jnp.einsum('shtj,jsl->tshl', weights.astype(jnp.bfloat16), key_rows, pref...  12.4 us
    dot_general x1, matrix products, shards(): jnp.einsum('necd,edf->necf', incoming, w_gate, preferred_element_type=jnp...  8.67 us
    reduce_sum x1, other arithmetic, fold_step(): new_sum = old_sum * factor + jnp.sum(weights, axis=3)  8.39 us
  transfers between devices with their start and end apart: 4, of which 3 were waited for; matrix products, arithmetic and copies ran while one was open for 14% of the time, Pallas kernels for 0%

commit v1 on v0

--- a/solution.py
+++ b/solution.py
@@ -91,7 +91,8 @@
         new_acc = old_acc * jnp.transpose(factor, (2, 0, 1))[..., None] + contrib
         return (new_max, new_sum, new_acc)
 
-    portion = lax.all_gather(latents, "expert", axis=1, tiled=True)
+    parts = lax.all_gather(latents, "expert", axis=0, tiled=False)
+    portion = jnp.concatenate(parts, axis=1)
     last_pos = jnp.max(own_pos)
     final_max, final_sum, final_acc = lax.cond(
         jnp.int32(0) <= last_pos,

time: 416 us -> 416 us (level)
  transfers between devices with their start and end apart: 4 -> 4, of which waited for: 3 -> 3; matrix products, arithmetic and copies ran while one was open for 14% -> 13% of each run, Pallas kernels for 0% -> 0%
where the time goes in v1:
time: 416 us; the launch traced here: 415 us
  waiting for transfers between devices  172 us (41%)
  blocking collectives  107 us (26%)
  matrix products  62.8 us (15%)
  local copies, waits for them, and re-layouts  32.3 us (8%)
  other arithmetic  15.4 us (4%)
  between operations  14.2 us (3%)
  starting transfers between devices  11.1 us (3%)
    all_to_all x1, blocking collectives, shards(): lax.all_to_all(outgoing, 'expert', split_axis=0, concat_axis=0, tiled=True)  107 us
    all_to_all x1, waiting for transfers between devices, shards(): lax.all_to_all(produced, 'expert', split_axis=0, concat_axis=0, tiled=True)  94.6 us
    all_gather x1, waiting for transfers between devices, shards(): parts = lax.all_gather(latents, 'expert', axis=0, tiled=False)  67.4 us
    dot_general x1, matrix products, fold_step(): jnp.einsum('tshl,jsl->shtj', query_rows, key_rows, preferred_element_type...  15.8 us
    dot_general x1, matrix products, shards(): jnp.einsum('necf,efd->necd', act, w_down, preferred_element_type=jnp.floa...  12.9 us
    all_gather x1, waiting for transfers between devices, shards(): lax.all_gather(w_out, 'dp', axis=0, tiled=True)  9.5 us
    reduce_sum x1, other arithmetic, fold_step(): new_sum = old_sum * factor + jnp.sum(weights, axis=3)  9.16 us
    dot_general x1, matrix products, shards(): jnp.einsum('necd,edf->necf', incoming, w_gate, preferred_element_type=jnp...  8.67 us
  transfers between devices with their start and end apart: 4, of which 3 were waited for; matrix products, arithmetic and copies ran while one was open for 13% of the time, Pallas kernels for 0%

profile of v1, /device:TPU:1, one launch (start us, length us, event | category | flops | bytes accessed | tf_op | source)
XLA Modules:
  0.0 415.4 jit_solution(4709314118830544687)
XLA Ops:
  9.0 2.1 broadcast_in_dim.29
  11.1 4.8 %all-to-all-start = ((bf16[4,2,512,128]{3,2,1,0:T(8,128)(2,1)}), bf16[4,2,512,128]{3,2,1,0:T(8,128)(2,1)}, u32[]{:S(2)}, u32[]{:S(2)}) async-start(bf16[4,2,512,128]{3,2,1,0:T(8,128)(2,1)} %broadcast_in_dim.29), calls=%async_computation | async-start | bytes 2097152 | tf_op jit(solution)/shard_map/all_to_all | solution.py:12
  16.4 2.6 reshape.152
  23.9 2.5 fusion.65
  26.7 2.7 convolution_bitcast_fusion
  29.9 67.4 %all-gather.6.cloned.1.call-done = bf16[64,64,2,512]{3,1,0,2:T(8,128)(2,1)} async-done(((bf16[1,64,2,512]{3,1,0,2:T(8,128)(2,1)}), bf16[64,64,2,512]{3,1,0,2:T(8,128)(2,1)}) %all-gather.6.cloned.1.call-update) | async-done | bytes 8388624 | tf_op jit(solution)/shard_map/all_gather | solution.py:94
  97.3 36.7 %conditional.1 = ((f32[2,8,64]{2,1,0:T(8,128)S(1)}, f32[64,2,8,512]{3,0,2,1:T(8,128)})) conditional(s32[]{:T(128)} %convert_element_type.74, (f32[2,8,64]{2,1,0:T(8,128)S(1)}, f32[64,2,8,512]{3,0,2,1:T(8,128)}) %tuple.12, (s32[64]{0:T(128)S(1)}, s32[1,2]{1,0:T(1,128)}, bf16[64,1,64,2,512]{4,2,0,3,1:T(8,128)(2,1)}, bf16[64,2,8,512]{3,2,1,0:T(8,128)(2,1)}, ...), branch_computations={%region_3.0_spmd, %region_4.7_spmd} | conditional | flops 8637918208 | bytes 125378928 | solution.py:97
  98.6 15.8 %fusion.2 = (f32[2,8,64]{2,1,0:T(8,128)}, f32[2,4096,64,8]{1,2,3,0:T(8,128)}) fusion(pred[2,64,4096]{2,1,0:T(8,128)(4,1)S(1)} %broadcast_and_fusion, bf16[4096,2,512,1]{2,0,3,1:T(8,128)(2,1)} %bitcast.157, bf16[64,2,8,512]{3,2,1,0:T(8,128)(2,1)} %get-tuple-element.57), kind=kOutput, calls=%fused_computation.4 | convolution fusion | flops 4307549184 | bytes 26742784 | tf_op jit(solution)/shard_map/cond/branch_1_fun/tshl,jsl->shtj/dot_general | solution.py:74
  115.1 9.2 %fusion.1 = f32[2,8,64]{2,1,0:T(8,128)S(1)} fusion(f32[2,4096,64,8]{1,2,3,0:T(8,128)} %get-tuple-element.61, f32[2,8,64]{2,1,0:T(8,128)S(1)} %get-tuple-element.59, pred[2,64,4096]{2,1,0:T(8,128)(4,1)S(1)} %broadcast_and_fusion), kind=kLoop, calls=%fused_computation.3 | loop fusion | flops 16776192 | bytes 17309696 | tf_op jit(solution)/shard_map/cond/branch_1_fun/reduce_sum | solution.py:84
  124.3 8.4 %bitcast_add_fusion = f32[64,2,8,512]{3,0,2,1:T(8,128)S(1)} fusion(f32[64,2,8,512]{3,0,2,1:T(8,128)S(1)} %copy-done.3, bf16[4096,2,512,1]{2,0,3,1:T(8,128)(2,1)S(1)} %bitcast.158, f32[2,4096,64,8]{1,2,3,0:T(8,128)} %get-tuple-element.61, f32[2,8,64]{2,1,0:T(8,128)S(1)} %get-tuple-element.59, pred[2,64,4096]{2,1,0:T(8,128)(4,1)S(1)} %broadcast_and_fusion, ...), kind=kOutput, calls=%fused_computation.10 | convolution fusion | flops 4312793088 | bytes 29892608 | tf_op jit(solution)/shard_map/cond/branch_1_fun/shtj,jsl->tshl/dot_general | solution.py:85
  134.0 2.4 fusion.44
  136.6 9.5 %all-gather.4.cloned.1.call-done = bf16[1024,2048]{1,0:T(8,128)(2,1)} async-done(((bf16[256,2048]{1,0:T(8,128)(2,1)}), bf16[1024,2048]{1,0:T(8,128)(2,1)}) %all-gather.4.cloned.1.call-update) | async-done | bytes 4194320 | tf_op jit(solution)/shard_map/all_gather | solution.py:113
  146.1 3.3 multiply_reduce_fusion
  150.4 3.0 convolution_convert_fusion
  153.4 6.0 %reshape.134 = bf16[64,1,14,2048]{3,2,0,1:T(8,128)(2,1)} reshape(bf16[896,2048]{1,0:T(8,128)(2,1)} %convolution_convert_fusion) | data formatting | bytes 7340032 | tf_op jit(solution)/shard_map/reshape | solution.py:142
  159.4 107.3 %all_to_all.15 = bf16[64,1,14,2048]{3,2,1,0:T(8,128)(2,1)S(1)} all-to-all(bf16[64,1,14,2048]{3,2,1,0:T(8,128)(2,1)} %bitcast.147), channel_id=1, replica_groups=mesh['dp'=4,'expert'=64] {'expert'}, dimensions={0} | all-to-all | bytes 7340032 | tf_op jit(solution)/shard_map/all_to_all | solution.py:143
  266.7 1.9 copy-done.2
  268.6 8.7 %fusion.18 = f32[64,14,704]{2,0,1:T(8,128)} fusion(bf16[64,1,14,2048]{3,2,1,0:T(8,128)(2,1)S(1)} %all_to_all.15, bf16[1,2048,704]{1,2,0:T(8,128)(2,1)S(1)} %copy-done.10), kind=kOutput, calls=%fused_computation.23 | convolution fusion | flops 2583691264 | bytes 9076736 | tf_op jit(solution)/shard_map/necd,edf->necf/dot_general | solution.py:144
  277.3 12.9 %convert_bitcast_fusion = bf16[64,1,14,2048]{3,0,2,1:T(8,128)(2,1)} fusion(bf16[1,704,2048]{2,1,0:T(8,128)(2,1)S(1)} %copy-done, bf16[1,2048,704]{1,2,0:T(8,128)(2,1)} %param.26, bf16[64,1,14,2048]{3,2,1,0:T(8,128)(2,1)} %copy-done.2, f32[64,14,704]{2,0,1:T(8,128)} %fusion.18), kind=kOutput, calls=%fused_computation.25 | convolution fusion | flops 5173002240 | bytes 15630336 | tf_op jit(solution)/shard_map/necf,efd->necd/dot_general | solution.py:147
  290.2 6.0 %copy.68 = bf16[64,1,14,2048]{3,2,1,0:T(8,128)(2,1)} copy(bf16[64,1,14,2048]{3,0,2,1:T(8,128)(2,1)} %convert_bitcast_fusion) | data formatting | bytes 7340032 | tf_op jit(solution)/shard_map/convert_element_type | solution.py:147
  296.2 6.2 %all-to-all-start.2 = ((bf16[64,1,14,2048]{3,2,1,0:T(8,128)(2,1)}), bf16[64,1,14,2048]{3,2,1,0:T(8,128)(2,1)}, u32[]{:S(2)}, u32[]{:S(2)}) async-start(bf16[64,1,14,2048]{3,2,1,0:T(8,128)(2,1)} %copy.68), calls=%async_computation.2 | async-start | bytes 8388608 | tf_op jit(solution)/shard_map/all_to_all | solution.py:150
  303.6 94.6 %all-to-all-done.2 = bf16[64,1,14,2048]{3,2,1,0:T(8,128)(2,1)} async-done(((bf16[64,1,14,2048]{3,2,1,0:T(8,128)(2,1)}), bf16[64,1,14,2048]{3,2,1,0:T(8,128)(2,1)}, u32[]{:S(2)}, u32[]{:S(2)}) %all-to-all-start.2) | async-done | bytes 3670048 | tf_op jit(solution)/shard_map/all_to_all | solution.py:150
  398.3 6.0 %reshape.140 = bf16[896,2048]{1,0:T(8,128)(2,1)} reshape(bf16[64,1,14,2048]{3,2,1,0:T(8,128)(2,1)} %all-to-all-done.2) | data formatting | bytes 7340032 | tf_op jit(solution)/shard_map/reshape | solution.py:151
  404.2 3.1 fusion.30
  (57 shorter events, 14.7 us)
Async XLA Ops:
  6.5 270.8 %copy-start = (bf16[1,704,2048]{2,1,0:T(8,128)(2,1)S(1)}, bf16[1,704,2048]{2,1,0:T(8,128)(2,1)}, u32[]{:S(2)}) copy-start(bf16[1,704,2048]{2,1,0:T(8,128)(2,1)} %param.27) | copy-start | bytes 8650756
  6.5 9.4 %copy-start.6 = (s32[1,64,2,6]{1,2,3,0:T(2,128)S(1)}, s32[1,64,2,6]{1,2,3,0:T(2,128)}, u32[]{:S(2)}) copy-start(s32[1,64,2,6]{1,2,3,0:T(2,128)} %param.20) | copy-start | bytes 9220
  6.5 13.8 %copy-start.5 = (bf16[1,64,2,2048]{3,2,1,0:T(2,128)(2,1)S(1)}, bf16[1,64,2,2048]{3,2,1,0:T(2,128)(2,1)}, u32[]{:S(2)}) copy-start(bf16[1,64,2,2048]{3,2,1,0:T(2,128)(2,1)} %param.15) | copy-start | bytes 1572868
  6.5 90.8 %all-gather.6.cloned.1.call-start = ((), (), s32[]{:S(2)}) async-start(), calls=%async_computation.4 | async-start | bytes 8519680 | tf_op jit(solution)/shard_map/all_gather | solution.py:94
  8.3 137.8 %all-gather.4.cloned.1.call-start = ((), (), s32[]{:S(2)}) async-start(), calls=%async_computation.3 | async-start | bytes 5242880 | tf_op jit(solution)/shard_map/all_gather | solution.py:113
  11.1 122.9 %all-to-all-start = ((bf16[4,2,512,128]{3,2,1,0:T(8,128)(2,1)}), bf16[4,2,512,128]{3,2,1,0:T(8,128)(2,1)}, u32[]{:S(2)}, u32[]{:S(2)}) async-start(bf16[4,2,512,128]{3,2,1,0:T(8,128)(2,1)} %broadcast_in_dim.29), calls=%async_computation | async-start | bytes 2097152 | tf_op jit(solution)/shard_map/all_to_all | solution.py:12
  16.0 10.7 %copy-start.7 = (bf16[2048]{0:T(1024)(128)(2,1)S(1)}, bf16[2048]{0:T(1024)(128)(2,1)}, u32[]{:S(2)}) copy-start(bf16[2048]{0:T(1024)(128)(2,1)} %param.22) | copy-start | bytes 12292
  115.1 9.2 %copy-start.3 = (f32[64,2,8,512]{3,0,2,1:T(8,128)S(1)}, f32[64,2,8,512]{3,0,2,1:T(8,128)}, u32[]{:S(2)}) copy-start(f32[64,2,8,512]{3,0,2,1:T(8,128)} %get-tuple-element.29) | copy-start | bytes 6291460 | tf_op jit(solution)/shard_map/cond
  115.1 9.2 %copy-start.9 = (bf16[64,1,64,2,512]{4,2,0,3,1:T(8,128)(2,1)S(1)}, bf16[64,1,64,2,512]{4,2,0,3,1:T(8,128)(2,1)}, u32[]{:S(2)}) copy-start(bf16[64,1,64,2,512]{4,2,0,3,1:T(8,128)(2,1)} %get-tuple-element.27) | copy-start | bytes 25165828 | tf_op jit(solution)/shard_map/cond
  132.7 1.4 copy-start.4
  149.4 1.0 copy-start.1
  159.4 109.2 %copy-start.10 = (bf16[1,2048,704]{1,2,0:T(8,128)(2,1)S(1)}, bf16[1,2048,704]{1,2,0:T(8,128)(2,1)}, u32[]{:S(2)}) copy-start(bf16[1,2048,704]{1,2,0:T(8,128)(2,1)} %param.25) | copy-start | bytes 8650756
  266.7 1.9 copy-start.2
  296.2 6.2 %copy-start.8 = (bf16[1,64,2,6]{1,2,3,0:T(2,128)(2,1)S(1)}, bf16[1,64,2,6]{1,2,3,0:T(2,128)(2,1)}, u32[]{:S(2)}) copy-start(bf16[1,64,2,6]{1,2,3,0:T(2,128)(2,1)} %param.21) | copy-start | bytes 4612
  296.2 102.0 %all-to-all-start.2 = ((bf16[64,1,14,2048]{3,2,1,0:T(8,128)(2,1)}), bf16[64,1,14,2048]{3,2,1,0:T(8,128)(2,1)}, u32[]{:S(2)}, u32[]{:S(2)}) async-start(bf16[64,1,14,2048]{3,2,1,0:T(8,128)(2,1)} %copy.68), calls=%async_computation.2 | async-start | bytes 8388608 | tf_op jit(solution)/shard_map/all_to_all | solution.py:150
Sparse Core Ops, SparseCore 0:
  10.1 87.1 all-gather.5
  99.1 46.9 all-gather.3
